TPU v7x, 32 devices: a whole 2x2x4 slice. The times are simulated.
32 devices in a mesh: fsdp: 16 (over z, x, core), tp: 2 (over y).
Axes of the slice: x: 2, y: 2, z: 4, core: 2. Of those that a mesh axis runs over, the one named last changes fastest.
Arguments:
- grad_iterate: bfloat16 [3584, 18432], P('tp', 'fsdp'), may hold values from -0.036828478 to 0.036828478
Outputs:
- update: float32 [3584, 18432], P('tp', 'fsdp')
All inputs are finite; a program needn't handle non-finite values.
Results may differ from a plain program's by a relative error of at most 0.0031.
Values may be sent and summed in bfloat16 or wider, within the bound.
A program may use at most 128 MiB of HBM per device.

v0:
```python
import functools
import math

import jax
import jax.numpy as jnp
from jax import lax
from jax.sharding import PartitionSpec as P

C = 18432


quintic_one = 3.4445
quintic_three = -4.775
quintic_five = 2.0315


def rows_by_rows(a, b):
    return lax.dot_general(a, b, (((1,), (1,)), ((), ())), preferred_element_type=jnp.float32)


def matmul(a, b):
    return jnp.dot(a, b, preferred_element_type=jnp.float32)


def general(grad_iterate):
    columns = lax.all_gather(grad_iterate, "tp", axis=0, tiled=True)
    shares = lax.psum_scatter(
        rows_by_rows(columns, grad_iterate), "fsdp", scatter_dimension=0, tiled=True
    )
    gram_cols = lax.all_gather(shares.astype(jnp.bfloat16), "fsdp", axis=0, tiled=True)
    applied = lax.dot_general(
        gram_cols, columns, (((0,), (0,)), ((), ())), preferred_element_type=jnp.float32
    )
    twice_applied = matmul(
        gram_cols.T, lax.all_gather(applied.astype(jnp.bfloat16), "tp", axis=0, tiled=True)
    )
    mixed = (
        quintic_one * grad_iterate.astype(jnp.float32)
        + quintic_three * applied
        + quintic_five * twice_applied
    )
    return mixed * math.sqrt(C)


def chunks_of(width):
    for count in (3, 2):
        if width % (count * 128) == 0:
            return count
    return 1


def paired(devices, own):
    rows, width = own.shape
    half = rows // 2
    piece = rows // (2 * devices)
    swap = [(0, 1), (1, 0)]
    first = lax.axis_index("tp") == 0

    def reduced(partial):
        share = lax.psum_scatter(partial, "fsdp", scatter_dimension=0, tiled=True)
        return share.astype(jnp.bfloat16)

    other = lax.ppermute(own, "tp", swap)

    left_share = reduced(rows_by_rows(own, own[:half]))
    corner_share = reduced(rows_by_rows(own[half:], own[half:]))

    picked = jnp.where(
        first,
        other.reshape(devices, 2, piece, width)[:, 0],
        own.reshape(devices, 2, piece, width)[:, 1],
    ).reshape(half, width)
    cross_share = reduced(rows_by_rows(picked, jnp.where(first, own, other)))
    cross_share = lax.all_gather(cross_share, "tp", axis=0, tiled=True)

    left = lax.all_gather(left_share, "fsdp", axis=0, tiled=True)
    corner = lax.all_gather(corner_share, "fsdp", axis=0, tiled=True)
    diagonal = jnp.concatenate(
        [left, jnp.concatenate([left[half:].T, corner], axis=0)], axis=1
    )
    cross = lax.all_gather(cross_share, "fsdp", axis=0, tiled=True)
    cross = jnp.where(first, cross.T, cross)

    count = chunks_of(width)
    step = width // count
    spans = [slice(i * step, (i + 1) * step) for i in range(count)]
    applied = [matmul(diagonal, own[:, s]) + matmul(cross, other[:, s]) for s in spans]
    low = [a.astype(jnp.bfloat16) for a in applied]
    far = [lax.ppermute(a, "tp", swap) for a in low]
    near = [matmul(diagonal, a) for a in low]
    out = []
    for i, s in enumerate(spans):
        twice = near[i] + matmul(cross, far[i])
        mixed = (
            quintic_one * own[:, s].astype(jnp.float32)
            + quintic_three * applied[i]
            + quintic_five * twice
        )
        out.append(mixed * math.sqrt(C))
    return jnp.concatenate(out, axis=1)


def solution(mesh):
    devices = mesh.shape["fsdp"]
    pair = mesh.shape["tp"] == 2

    def local(grad_iterate):
        if pair and grad_iterate.shape[0] % (2 * devices) == 0:
            return paired(devices, grad_iterate)
        return general(grad_iterate)

    return jax.shard_map(
        local,
        mesh=mesh,
        in_specs=(P("tp", "fsdp"),),
        out_specs=P("tp", "fsdp"),
        check_vma=False,
    )
```

profile of v0, /device:TPU:28, one launch (start us, length us, event | category | flops | bytes accessed | tf_op | source)
XLA Modules:
  0.0 552.9 jit_solution(13139247162025827451)
XLA Ops:
  6.5 10.4 %fusion.14 = f32[1792,896]{1,0:T(8,128)} fusion(bf16[1792,1152]{1,0:T(8,128)(2,1)} %param.1), kind=kOutput, calls=%fused_computation.24 | convolution fusion | flops 3699376128 | bytes 12615680 | tf_op jit(solution)/shard_map/dot_general | solution.py:18
  17.0 0.0 reduce-scatter.10.cloned.1.call-start
  17.0 0.6 collective-permute-start
  17.6 6.3 %fusion.12 = f32[896,896]{1,0:T(8,128)} fusion(bf16[1792,1152]{1,0:T(8,128)(2,1)} %param.1), kind=kOutput, calls=%fused_computation.22 | convolution fusion | flops 1849688064 | bytes 5275648 | tf_op jit(solution)/shard_map/dot_general | solution.py:18
  24.0 0.0 reduce-scatter.8.cloned.1.call-start
  24.0 84.3 %collective-permute-done = bf16[1792,1152]{1,0:T(8,128)(2,1)} collective-permute-done((bf16[1792,1152]{1,0:T(8,128)(2,1)}, bf16[1792,1152]{1,0:T(8,128)(2,1)}, u32[]{:S(2)}, u32[]{:S(2)}) %collective-permute-start) | collective-permute-done | bytes 4128800 | tf_op jit(solution)/shard_map/ppermute | solution.py:63
  108.3 2.6 slice_select_fusion
  110.9 0.8 copy-done
  111.7 8.8 %fusion = f32[896,1792]{1,0:T(8,128)} fusion(bf16[896,1152]{1,0:T(8,128)(2,1)S(1)} %bitcast.22, bf16[1792,1152]{1,0:T(8,128)(2,1)S(1)} %copy-done, bf16[1792,1152]{1,0:T(8,128)(2,1)} %collective-permute-done, pred[]{:T(512)S(6)} %eq.3), kind=kOutput, calls=%fused_computation.3 | convolution fusion | flops 3701440512 | bytes 16744449 | tf_op jit(solution)/shard_map/dot_general | solution.py:18
  120.6 0.0 all-gather.4.cloned.1.call-start
  120.6 0.0 reduce-scatter.6.cloned.1.call-done
  120.7 1.8 convert_element_type.28
  122.4 0.0 all-gather.6.cloned.1.call-start
  122.5 51.0 %reduce-scatter.10.cloned.1.call-done = f32[56,896]{1,0:T(8,128)} async-done(((f32[896,896]{1,0:T(8,128)}), f32[56,896]{1,0:T(8,128)}) %reduce-scatter.10.cloned.1.call-update) | async-done | bytes 200720
  173.5 1.6 convert_element_type.29
  175.1 0.0 all-gather.8.cloned.1.call-start
  175.1 87.2 %reduce-scatter.8.cloned.1.call-done = f32[56,1792]{1,0:T(8,128)} async-done(((f32[896,1792]{1,0:T(8,128)}), f32[56,1792]{1,0:T(8,128)}) %reduce-scatter.8.cloned.1.call-update) | async-done | bytes 401424 | tf_op jit(solution)/shard_map/reduce_scatter | solution.py:60
  262.3 1.0 convert_element_type.30
  263.3 7.0 %all_gather.14 = bf16[112,1792]{1,0:T(8,128)(2,1)} all-gather(bf16[56,1792]{1,0:T(8,128)(2,1)S(1)} %convert_element_type.30), channel_id=1, replica_groups=mesh['fsdp'=16,'tp'=2] {'tp'}, dimensions={0}, use_global_device_ids=true | all-gather | bytes 602112 | tf_op jit(solution)/shard_map/all_gather | solution.py:74
  270.3 0.0 all-gather.8.cloned.1.call-update
  270.3 3.7 fusion.28
  274.1 2.5 copy.14
  276.6 1.6 copy.16
  278.2 1.6 copy.17
  279.8 29.5 %all-gather.4.cloned.1.call-done = bf16[1792,896]{1,0:T(8,128)(2,1)} async-done(((bf16[112,896]{1,0:T(8,128)(2,1)}), bf16[1792,896]{1,0:T(8,128)(2,1)}) %all-gather.4.cloned.1.call-update) | async-done | bytes 3211280 | tf_op jit(solution)/shard_map/all_gather | solution.py:76
  309.3 1.4 slice-done
  310.7 2.3 copy.15
  313.0 36.7 %all-gather.6.cloned.1.call-done = bf16[896,896]{1,0:T(8,128)(2,1)} async-done(((bf16[56,896]{1,0:T(8,128)(2,1)}), bf16[896,896]{1,0:T(8,128)(2,1)}) %all-gather.6.cloned.1.call-update) | async-done | bytes 1605648 | tf_op jit(solution)/shard_map/all_gather | solution.py:77
  349.7 7.6 %fusion.21 = f32[1792,384]{0,1:T(8,128)} fusion(bf16[1792,1152]{1,0:T(8,128)(2,1)} %param.1, bf16[896,896]{1,0:T(8,128)(2,1)} %all-gather.6.cloned.1.call-done, bf16[896,896]{1,0:T(8,128)(2,1)} %bitcast.23, bf16[1792,896]{1,0:T(8,128)(2,1)} %all-gather.4.cloned.1.call-done), kind=kOutput, calls=%fused_computation.31 | convolution fusion | flops 2485518336 | bytes 10551296 | tf_op jit(solution)/shard_map/dot_general | solution.py:22
  357.4 4.3 fusion.19
  361.7 4.5 fusion.23
  366.2 46.5 %all-gather.8.cloned.1.call-done = bf16[1792,1792]{1,0:T(8,128)(2,1)} async-done(((bf16[112,1792]{1,0:T(8,128)(2,1)}), bf16[1792,1792]{1,0:T(8,128)(2,1)}) %all-gather.8.cloned.1.call-update) | async-done | bytes 6422544 | tf_op jit(solution)/shard_map/all_gather | solution.py:81
  412.7 10.0 %copy.10 = bf16[1792,1792]{0,1:T(8,128)(2,1)} copy(bf16[1792,1792]{1,0:T(8,128)(2,1)} %all-gather.8.cloned.1.call-done) | data formatting | bytes 12845056 | tf_op jit(solution)/shard_map/all_gather | solution.py:81
  422.7 8.1 %bitcast_select_fusion = bf16[1792,1792]{1,0:T(8,128)(2,1)} fusion(bf16[1792,1792]{1,0:T(8,128)(2,1)} %all-gather.8.cloned.1.call-done, bf16[1792,1792]{0,1:T(8,128)(2,1)} %copy.10, pred[]{:T(512)S(6)} %eq.3), kind=kLoop, calls=%fused_computation.2 | loop fusion | flops 3211264 | bytes 19267584 | tf_op jit(solution)/shard_map/jit(_where)/select_n | solution.py:82
  430.8 8.4 %fusion.30 = (bf16[1792,384]{0,1:T(8,128)(2,1)S(1)}, f32[1792,384]{0,1:T(8,128)}) fusion(f32[1792,384]{0,1:T(8,128)} %fusion.21, bf16[1792,1792]{1,0:T(8,128)(2,1)} %bitcast_select_fusion, bf16[1792,1152]{1,0:T(8,128)(2,1)} %collective-permute-done), kind=kOutput, calls=%fused_computation.40 | convolution fusion | flops 2467627008 | bytes 14680064 | tf_op jit(solution)/shard_map/dot_general | solution.py:22
  439.2 5.6 %fusion.29 = (bf16[1792,384]{0,1:T(8,128)(2,1)S(1)}, f32[1792,384]{0,1:T(8,128)}) fusion(f32[1792,384]{0,1:T(8,128)S(1)} %copy-done.14, bf16[1792,1792]{1,0:T(8,128)(2,1)S(1)} %copy-done.2, bf16[1792,1152]{1,0:T(8,128)(2,1)} %collective-permute-done), kind=kOutput, calls=%fused_computation.39 | convolution fusion | flops 2467627008 | bytes 14680064 | tf_op jit(solution)/shard_map/dot_general | solution.py:22
  444.8 2.0 collective-permute-start.3
  446.8 4.9 fusion.31
  451.8 0.2 collective-permute-start.1
  452.0 15.4 %fusion.26 = f32[1792,384]{0,1:T(8,128)} fusion(bf16[1792,384]{0,1:T(8,128)(2,1)S(1)} %get-tuple-element.10, bf16[896,896]{1,0:T(8,128)(2,1)S(1)} %copy-done.10, bf16[896,896]{1,0:T(8,128)(2,1)S(1)} %bitcast.26, bf16[1792,896]{1,0:T(8,128)(2,1)S(1)} %copy-done.3), kind=kOutput, calls=%fused_computation.36 | convolution fusion | flops 2485518336 | bytes 10551296 | tf_op jit(solution)/shard_map/dot_general | solution.py:22
  467.4 15.6 %fusion.25 = f32[1792,384]{0,1:T(8,128)} fusion(bf16[1792,384]{0,1:T(8,128)(2,1)S(1)} %get-tuple-element.8, bf16[896,896]{1,0:T(8,128)(2,1)S(1)} %copy-done.10, bf16[896,896]{1,0:T(8,128)(2,1)S(1)} %bitcast.27, bf16[1792,896]{1,0:T(8,128)(2,1)S(1)} %copy-done.3), kind=kOutput, calls=%fused_computation.35 | convolution fusion | flops 2485518336 | bytes 10551296 | tf_op jit(solution)/shard_map/dot_general | solution.py:22
  483.0 15.3 %fusion.27 = f32[1792,384]{0,1:T(8,128)} fusion(bf16[1792,384]{0,1:T(8,128)(2,1)S(1)} %get-tuple-element.12, bf16[896,896]{1,0:T(8,128)(2,1)S(1)} %copy-done.10, bf16[896,896]{1,0:T(8,128)(2,1)S(1)} %bitcast.28, bf16[1792,896]{1,0:T(8,128)(2,1)S(1)} %copy-done.3), kind=kOutput, calls=%fused_computation.37 | convolution fusion | flops 2485518336 | bytes 10551296 | tf_op jit(solution)/shard_map/dot_general | solution.py:22
  498.4 6.7 %fusion.8 = f32[1792,384]{0,1:T(8,128)S(1)} fusion(f32[1792,384]{0,1:T(8,128)} %fusion.26, bf16[1792,1792]{1,0:T(8,128)(2,1)S(1)} %copy-done.2, bf16[1792,384]{0,1:T(8,128)(2,1)S(1)} %collective-permute-done.2, f32[1792,384]{0,1:T(8,128)} %get-tuple-element.11, bf16[1792,384]{0,1:T(8,128)(2,1)S(1)} %copy-done.8), kind=kOutput, calls=%fused_computation.14 | convolution fusion | flops 2471755776 | bytes 17432576 | tf_op jit(solution)/shard_map/dot_general | solution.py:22
  505.1 3.0 fusion.5
  508.1 22.4 %collective-permute-done.1 = bf16[1792,384]{0,1:T(8,128)(2,1)S(1)} collective-permute-done((bf16[1792,384]{0,1:T(8,128)(2,1)S(1)}, bf16[1792,384]{0,1:T(8,128)(2,1)S(1)}, u32[]{:S(2)}, u32[]{:S(2)}) %collective-permute-start.1) | collective-permute-done | bytes 1376288 | tf_op jit(solution)/shard_map/ppermute | solution.py:89
  530.5 2.9 fusion.11
  533.5 3.5 pad_maximum_fusion
  537.0 8.8 %copy.13 = f32[1792,1152]{1,0:T(8,128)} copy(f32[1792,1152]{0,1:T(8,128)} %pad_maximum_fusion) | data formatting | bytes 16515072 | tf_op jit(solution)/shard_map/concatenate | solution.py:100
  (39 shorter events, 0.2 us)
Async XLA Ops:
  6.5 114.1 %reduce-scatter.6.cloned.1.call-start = ((), (), s32[]{:S(2)}) async-start(), calls=%async_computation.3 | async-start | bytes 6823936 | tf_op jit(solution)/shard_map/reduce_scatter | solution.py:60
  17.0 156.5 %reduce-scatter.10.cloned.1.call-start = ((), (), s32[]{:S(2)}) async-start(), calls=%async_computation.8 | async-start | bytes 3411968
  17.0 91.3 %collective-permute-start = (bf16[1792,1152]{1,0:T(8,128)(2,1)}, bf16[1792,1152]{1,0:T(8,128)(2,1)}, u32[]{:S(2)}, u32[]{:S(2)}) collective-permute-start(bf16[1792,1152]{1,0:T(8,128)(2,1)} %param.1), channel_id=1, source_target_pairs={{0,1},{1,0},{2,3},{3,2},{4,5},{5,4},{6,7},{7,6},{8,9},{9,8},{10,11... | collective-permute-start | bytes 12386312 | tf_op jit(solution)/shard_map/ppermute | solution.py:63
  24.0 238.3 %reduce-scatter.8.cloned.1.call-start = ((), (), s32[]{:S(2)}) async-start(), calls=%async_computation.6 | async-start | bytes 6823936 | tf_op jit(solution)/shard_map/reduce_scatter | solution.py:60
  108.3 3.4 copy-start
  120.6 188.7 %all-gather.4.cloned.1.call-start = ((), (), s32[]{:S(2)}) async-start(), calls=%async_computation.4 | async-start | bytes 3411968 | tf_op jit(solution)/shard_map/all_gather | solution.py:76
  122.4 227.3 %all-gather.6.cloned.1.call-start = ((), (), s32[]{:S(2)}) async-start(), calls=%async_computation.5 | async-start | bytes 1705984 | tf_op jit(solution)/shard_map/all_gather | solution.py:77
  175.1 237.6 %all-gather.8.cloned.1.call-start = ((), (), s32[]{:S(2)}) async-start(), calls=%async_computation.7 | async-start | bytes 6823936 | tf_op jit(solution)/shard_map/all_gather | solution.py:81
  309.3 1.4 slice-start
  349.7 7.6 %copy-start.1 = (bf16[1792,1152]{1,0:T(8,128)(2,1)S(1)}, bf16[1792,1152]{1,0:T(8,128)(2,1)}, u32[]{:S(2)}) copy-start(bf16[1792,1152]{1,0:T(8,128)(2,1)} %param.1) | copy-start | bytes 12386308
  349.7 7.6 %copy-start.3 = (bf16[1792,896]{1,0:T(8,128)(2,1)S(1)}, bf16[1792,896]{1,0:T(8,128)(2,1)}, u32[]{:S(2)}) copy-start(bf16[1792,896]{1,0:T(8,128)(2,1)} %all-gather.4.cloned.1.call-done) | copy-start | bytes 9633796
  349.7 7.6 %copy-start.4 = (bf16[896,896]{0,1:T(8,128)(2,1)S(1)}, bf16[896,896]{0,1:T(8,128)(2,1)}, u32[]{:S(2)}) copy-start(bf16[896,896]{0,1:T(8,128)(2,1)} %copy.15) | copy-start | bytes 4816900
  349.7 7.6 %copy-start.9 = (bf16[896,896]{1,0:T(8,128)(2,1)S(1)}, bf16[896,896]{1,0:T(8,128)(2,1)}, u32[]{:S(2)}) copy-start(bf16[896,896]{1,0:T(8,128)(2,1)} %all-gather.6.cloned.1.call-done) | copy-start | bytes 4816900
  430.8 8.5 %copy-start.2 = (bf16[1792,1792]{1,0:T(8,128)(2,1)S(1)}, bf16[1792,1792]{1,0:T(8,128)(2,1)}, u32[]{:S(2)}) copy-start(bf16[1792,1792]{1,0:T(8,128)(2,1)} %bitcast_select_fusion) | copy-start | bytes 19267588
  430.8 8.5 %copy-start.14 = (f32[1792,384]{0,1:T(8,128)S(1)}, f32[1792,384]{0,1:T(8,128)}, u32[]{:S(2)}) copy-start(f32[1792,384]{0,1:T(8,128)} %fusion.19) | copy-start | bytes 8257540
  439.2 59.1 %collective-permute-start.2 = (bf16[1792,384]{0,1:T(8,128)(2,1)S(1)}, bf16[1792,384]{0,1:T(8,128)(2,1)S(1)}, u32[]{:S(2)}, u32[]{:S(2)}) collective-permute-start(bf16[1792,384]{0,1:T(8,128)(2,1)S(1)} %get-tuple-element.10), channel_id=1, source_target_pairs={{0,1},{1,0},{2,3},{3,2},{4,5},{5,4},{6,7},{7,6},{8,9},{9,8},{10,11... | collective-permute-start | bytes 4128776 | tf_op jit(solution)/shard_map/ppermute | solution.py:89
  444.8 7.2 %copy-start.5 = (bf16[896,896]{0,1:T(8,128)(2,1)S(1)}, bf16[896,896]{0,1:T(8,128)(2,1)}, u32[]{:S(2)}) copy-start(bf16[896,896]{0,1:T(8,128)(2,1)} %copy.15) | copy-start | bytes 4816900
  444.8 7.2 %copy-start.10 = (bf16[896,896]{1,0:T(8,128)(2,1)S(1)}, bf16[896,896]{1,0:T(8,128)(2,1)}, u32[]{:S(2)}) copy-start(bf16[896,896]{1,0:T(8,128)(2,1)} %all-gather.6.cloned.1.call-done) | copy-start | bytes 4816900
  444.8 60.3 %collective-permute-start.3 = (bf16[1792,384]{0,1:T(8,128)(2,1)S(1)}, bf16[1792,384]{0,1:T(8,128)(2,1)S(1)}, u32[]{:S(2)}, u32[]{:S(2)}) collective-permute-start(bf16[1792,384]{0,1:T(8,128)(2,1)S(1)} %get-tuple-element.8), channel_id=1, source_target_pairs={{0,1},{1,0},{2,3},{3,2},{4,5},{5,4},{6,7},{7,6},{8,9},{9,8},{10,11... | collective-permute-start | bytes 4128776 | tf_op jit(solution)/shard_map/ppermute | solution.py:89
  451.8 78.8 %collective-permute-start.1 = (bf16[1792,384]{0,1:T(8,128)(2,1)S(1)}, bf16[1792,384]{0,1:T(8,128)(2,1)S(1)}, u32[]{:S(2)}, u32[]{:S(2)}) collective-permute-start(bf16[1792,384]{0,1:T(8,128)(2,1)S(1)} %get-tuple-element.12), channel_id=1, source_target_pairs={{0,1},{1,0},{2,3},{3,2},{4,5},{5,4},{6,7},{7,6},{8,9},{9,8},{10,11... | collective-permute-start | bytes 4128776 | tf_op jit(solution)/shard_map/ppermute | solution.py:89
  483.0 15.3 %copy-start.8 = (bf16[1792,384]{0,1:T(8,128)(2,1)S(1)}, bf16[1792,384]{0,1:T(8,128)(2,1)}, u32[]{:S(2)}) copy-start(bf16[1792,384]{0,1:T(8,128)(2,1)} %copy.16) | copy-start | bytes 4128772
  498.3 6.8 %copy-start.7 = (bf16[1792,384]{0,1:T(8,128)(2,1)S(1)}, bf16[1792,384]{0,1:T(8,128)(2,1)}, u32[]{:S(2)}) copy-start(bf16[1792,384]{0,1:T(8,128)(2,1)} %copy.17) | copy-start | bytes 4128772
  498.3 6.8 %copy-start.11 = (f32[1792,384]{0,1:T(8,128)S(1)}, f32[1792,384]{0,1:T(8,128)}, u32[]{:S(2)}) copy-start(f32[1792,384]{0,1:T(8,128)} %get-tuple-element.9) | copy-start | bytes 8257540
  498.3 6.8 %copy-start.13 = (f32[1792,384]{0,1:T(8,128)S(1)}, f32[1792,384]{0,1:T(8,128)}, u32[]{:S(2)}) copy-start(f32[1792,384]{0,1:T(8,128)} %fusion.25) | copy-start | bytes 8257540
  505.1 25.4 %copy-start.6 = (bf16[1792,384]{0,1:T(8,128)(2,1)S(1)}, bf16[1792,384]{0,1:T(8,128)(2,1)}, u32[]{:S(2)}) copy-start(bf16[1792,384]{0,1:T(8,128)(2,1)} %copy.14) | copy-start | bytes 4128772
  505.1 25.4 %copy-start.12 = (f32[1792,384]{0,1:T(8,128)S(1)}, f32[1792,384]{0,1:T(8,128)}, u32[]{:S(2)}) copy-start(f32[1792,384]{0,1:T(8,128)} %fusion.27) | copy-start | bytes 8257540
Sparse Core Ops, SparseCore 0:
  17.1 85.2 reduce-scatter.5
  106.3 67.1 reduce-scatter.9
  177.4 84.8 reduce-scatter.7
  264.3 44.9 all-gather.3
  311.3 38.4 all-gather.5
  351.9 60.7 all-gather.7
where the time goes:
time: 563 us; the launch traced here: 553 us
  waiting for transfers between devices  358 us (64%)
  matrix products  120 us (21%)
  local copies, waits for them, and re-layouts  32.9 us (6%)
  other arithmetic  18.5 us (3%)
  between operations  13.9 us (2%)
  blocking collectives  7 us (1%)
    dot_general x12, matrix products, matmul(): return jnp.dot(a, b, preferred_element_type=jnp.float32)  94.3 us
    reduce_scatter x2, waiting for transfers between devices, reduced(): share = lax.psum_scatter(partial, 'fsdp', scatter_dimension=0, tiled=True)  87.2 us
    ppermute x1, waiting for transfers between devices, paired(): other = lax.ppermute(own, 'tp', swap)  84.3 us
    unnamed x7, waiting for transfers between devices  51.1 us
    all_gather x1, waiting for transfers between devices, paired(): cross = lax.all_gather(cross_share, 'fsdp', axis=0, tiled=True)  46.5 us
    all_gather x1, waiting for transfers between devices, paired(): corner = lax.all_gather(corner_share, 'fsdp', axis=0, tiled=True)  36.7 us
    all_gather x1, waiting for transfers between devices, paired(): left = lax.all_gather(left_share, 'fsdp', axis=0, tiled=True)  29.5 us
    dot_general x3, matrix products, rows_by_rows(): lax.dot_general(a, b, (((1,), (1,)), ((), ())), preferred_element_type=jn...  25.6 us
  transfers between devices with their start and end apart: 10, of which 7 were waited for; matrix products, arithmetic and copies ran while one was open for 21% of the time, Pallas kernels for 0%

commit v1 on v0

v1 whole, which is shorter than its diff:
```python
import functools
import math

import jax
import jax.numpy as jnp
from jax import lax
from jax.experimental import pallas as pl
from jax.experimental.pallas import tpu as pltpu
from jax.sharding import PartitionSpec as P

quintic_one = 3.4445
quintic_three = -4.775
quintic_five = 2.0315

MESH = pl.DeviceIdType.MESH


def rows_by_rows(a, b):
    return lax.dot_general(a, b, (((1,), (1,)), ((), ())), preferred_element_type=jnp.float32)


def matmul(a, b):
    return jnp.dot(a, b, preferred_element_type=jnp.float32)


def general(grad_iterate, scale):
    columns = lax.all_gather(grad_iterate, "tp", axis=0, tiled=True)
    shares = lax.psum_scatter(
        rows_by_rows(columns, grad_iterate), "fsdp", scatter_dimension=0, tiled=True
    )
    gram_cols = lax.all_gather(shares.astype(jnp.bfloat16), "fsdp", axis=0, tiled=True)
    applied = lax.dot_general(
        gram_cols, columns, (((0,), (0,)), ((), ())), preferred_element_type=jnp.float32
    )
    twice_applied = matmul(
        gram_cols.T, lax.all_gather(applied.astype(jnp.bfloat16), "tp", axis=0, tiled=True)
    )
    mixed = (
        quintic_one * grad_iterate.astype(jnp.float32)
        + quintic_three * applied
        + quintic_five * twice_applied
    )
    return mixed * scale


def fused_kernel(
    nz, tile, scale,
    x_hbm, o_hbm,
    xg, xp, gram, out, cown, dxs, dxr, dzs, dzr, cxs, cxr, czs, czr,
    local_sem, ys, yr, cs, cr, dx_s, dx_r, dz_s, dz_r, cx_s, cx_r, cz_s, cz_r,
    daz_s, daz_r, dax_s, dax_r, dac_s, dac_r, day_s, day_r, dat_s, dat_r,
    cay_s, cay_r, caz_s, caz_r, cax_s, cax_r, cac_s, cac_r, out_sem,
):
    f = lax.axis_index("fsdp")
    y = lax.axis_index("tp")
    c = lax.rem(f, 2)
    xx = lax.rem(f // 2, 2)
    z = f // 4

    rows, width = xg.shape[1], xg.shape[2]
    half = rows // 2
    quarter = half // 2
    dpiece = half // nz
    cpiece = quarter // nz

    def device(z_, x_, c_, y_):
        return (z_ * 4 + x_ * 2 + c_, y_)

    to_y = device(z, xx, c, 1 - y)
    to_x = device(z, 1 - xx, c, y)
    to_c = device(z, xx, 1 - c, y)
    to_z = [device(lax.rem(z + k, nz), xx, c, y) for k in range(1, nz)]

    def remote(src, dst, ssem, rsem, target):
        return pltpu.make_async_remote_copy(
            src_ref=src, dst_ref=dst, send_sem=ssem, recv_sem=rsem,
            device_id=target, device_id_type=MESH,
        )

    load = pltpu.make_async_copy(x_hbm, xg.at[y], local_sem)
    load.start()
    barrier = pltpu.get_barrier_semaphore()
    peers = [to_y, to_x, to_c] + to_z
    for peer in peers:
        pl.semaphore_signal(barrier, inc=1, device_id=peer, device_id_type=MESH)
    pl.semaphore_wait(barrier, len(peers))
    load.wait()

    sends = []

    def begin(copy):
        copy.start()
        sends.append(copy)
        return copy

    def al(i, m):
        return pl.multiple_of(i, m)

    share = begin(remote(xg.at[y], xp.at[y], cs.at[0], cr.at[0], to_c))
    over = []
    for s in range(2):
        h = (1 - y) if s == 0 else y
        block = xg.at[y, pl.ds(al(h * half, half), half)]
        over.append(begin(remote(block, block, ys.at[s], yr.at[s], to_y)))
    share.wait_recv()

    cols = pl.ds(al(c * half, half), half)

    def gram_part(left, lrow, n, right, rrow):
        l = pl.ds(lrow, n)
        r = pl.ds(rrow, half)
        return rows_by_rows(xg[left, l, :], xg[right, r, :]) + rows_by_rows(
            xp[left, l, :], xp[right, r, :]
        )

    def order(p):
        return lax.rem(z + 1 + p, nz)

    chalf = al(c * half, half)

    def d_copy(p):
        t = order(p)
        return remote(dxs.at[t], dxr.at[t], dx_s.at[p], dx_r.at[p], to_x)

    def d_send(p, _):
        t = order(p)
        dxs[t] = gram_part(y, al((1 - xx) * half + t * dpiece, dpiece), dpiece, y, chalf).astype(
            jnp.bfloat16
        )
        d_copy(p).start()
        return 0

    lax.fori_loop(0, nz, d_send, 0)

    def d_own(p, _):
        t = order(p)
        out[pl.ds(al(t * dpiece, dpiece), dpiece), 0:half] = gram_part(
            y, al(xx * half + t * dpiece, dpiece), dpiece, y, chalf
        )
        return 0

    lax.fori_loop(0, nz, d_own, 0)

    dz = []
    for p in range(nz):
        t = order(p)
        d_copy(p).wait()
        place = pl.ds(al(t * dpiece, dpiece), dpiece)
        total = out[place, 0:half] + dxr[t].astype(jnp.float32)
        if p < nz - 1:
            dzs[p] = total.astype(jnp.bfloat16)
            dz.append(begin(remote(dzs.at[p], dzr.at[p], dz_s.at[p], dz_r.at[p], to_z[p])))
        else:
            out[place, 0:half] = total
    total = out[pl.ds(al(z * dpiece, dpiece), dpiece), 0:half]
    for p in range(nz - 1):
        dz[p].wait_recv()
        total = total + dzr[p].astype(jnp.float32)

    def d_slab(who, x_, z_):
        return gram.at[3 * who, pl.ds(al(x_ * half + z_ * dpiece, dpiece), dpiece), cols]

    gram[3 * y, pl.ds(al(xx * half + z * dpiece, dpiece), dpiece), cols] = total.astype(
        jnp.bfloat16
    )

    mine = d_slab(y, xx, z)
    daz = [
        begin(remote(mine, mine, daz_s.at[k], daz_r.at[k], to_z[k])) for k in range(nz - 1)
    ]
    dax, dac, day = [], [], []
    for k in range(nz):
        if k > 0:
            daz[k - 1].wait_recv()
        here = d_slab(y, xx, lax.rem(z - k + nz, nz))
        dax.append(begin(remote(here, here, dax_s.at[k], dax_r.at[k], to_x)))
        dac.append(begin(remote(here, here, dac_s.at[k], dac_r.at[k], to_c)))
        day.append(begin(remote(here, here, day_s.at[k], day_r.at[k], to_y)))

    for s in range(2):
        over[s].wait_recv()
    fwd = (1 - y) * (1 - c) + y
    block = pl.ds(al(fwd * half, half), half)
    cfwd = begin(remote(xg.at[1 - y, block], xp.at[1 - y, block], cs.at[1], cr.at[1], to_c))
    cfwd.wait_recv()

    def c_copy(p):
        t = order(p)
        return remote(cxs.at[t], cxr.at[t], cx_s.at[p], cx_r.at[p], to_x)

    def c_send(p, _):
        t = order(p)
        cxs[t] = gram_part(
            0, al(y * half + (1 - xx) * quarter + t * cpiece, cpiece), cpiece, 1, chalf
        ).astype(jnp.bfloat16)
        c_copy(p).start()
        return 0

    lax.fori_loop(0, nz, c_send, 0)

    def c_own(p, _):
        t = order(p)
        cown[t] = gram_part(
            0, al(y * half + xx * quarter + t * cpiece, cpiece), cpiece, 1, chalf
        )
        return 0

    lax.fori_loop(0, nz, c_own, 0)

    cz = []
    for p in range(nz):
        t = order(p)
        c_copy(p).wait()
        total = cown[t] + cxr[t].astype(jnp.float32)
        if p < nz - 1:
            czs[p] = total.astype(jnp.bfloat16)
            cz.append(begin(remote(czs.at[p], czr.at[p], cz_s.at[p], cz_r.at[p], to_z[p])))
        else:
            cown[t] = total

    for k in range(nz):
        dax[k].wait_recv()
        here = d_slab(y, 1 - xx, lax.rem(z - k + nz, nz))
        dac.append(begin(remote(here, here, dac_s.at[nz + k], dac_r.at[nz + k], to_c)))

    total = cown[z]
    for p in range(nz - 1):
        cz[p].wait_recv()
        total = total + czr[p].astype(jnp.float32)

    def c_slab(who, x_, z_):
        return gram.at[
            1, pl.ds(al(who * half + x_ * quarter + z_ * cpiece, cpiece), cpiece), cols
        ]

    gram[1, pl.ds(al(y * half + xx * quarter + z * cpiece, cpiece), cpiece), cols] = total.astype(
        jnp.bfloat16
    )
    mine = c_slab(y, xx, z)
    cay = begin(remote(mine, mine, cay_s, cay_r, to_y))
    caz, cax, cac = [], [], []
    for k in range(nz - 1):
        caz.append(begin(remote(mine, mine, caz_s.at[k], caz_r.at[k], to_z[k])))
    cax.append(begin(remote(mine, mine, cax_s.at[0], cax_r.at[0], to_x)))
    cac.append(begin(remote(mine, mine, cac_s.at[0], cac_r.at[0], to_c)))
    cay.wait_recv()
    theirs = c_slab(1 - y, xx, z)
    for k in range(nz - 1):
        j = nz - 1 + k
        caz.append(begin(remote(theirs, theirs, caz_s.at[j], caz_r.at[j], to_z[k])))
    cax.append(begin(remote(theirs, theirs, cax_s.at[1], cax_r.at[1], to_x)))
    cac.append(begin(remote(theirs, theirs, cac_s.at[1], cac_r.at[1], to_c)))
    for k in range(nz):
        here = d_slab(y, 1 - xx, lax.rem(z - k + nz, nz))
        day.append(begin(remote(here, here, day_s.at[nz + k], day_r.at[nz + k], to_y)))

    for copy in dac:
        copy.wait_recv()

    def tile_of(i):
        return pl.ds(al(i * tile, tile), tile)

    def first(i, _):
        m = tile_of(i)
        out[m, :] = matmul(gram[3 * y, m, :], xg[y])
        return 0

    lax.fori_loop(0, rows // tile, first, 0)

    n = 2
    for k in range(1, nz):
        for w in range(2):
            caz[w * (nz - 1) + k - 1].wait_recv()
            who = y if w == 0 else 1 - y
            here = c_slab(who, xx, lax.rem(z - k + nz, nz))
            cax.append(begin(remote(here, here, cax_s.at[n], cax_r.at[n], to_x)))
            cac.append(begin(remote(here, here, cac_s.at[n], cac_r.at[n], to_c)))
            n += 1
    dat = []
    for k in range(nz):
        day[k].wait_recv()
        here = d_slab(1 - y, xx, lax.rem(z - k + nz, nz))
        dat.append(begin(remote(here, here, dat_s.at[k], dat_r.at[k], to_c)))
    for j in range(2 * nz):
        cax[j].wait_recv()
        k, w = j // 2, j % 2
        who = y if w == 0 else 1 - y
        here = c_slab(who, 1 - xx, lax.rem(z - k + nz, nz))
        cac.append(begin(remote(here, here, cac_s.at[n], cac_r.at[n], to_c)))
        n += 1
    for copy in cac:
        copy.wait_recv()

    def flip(i, _):
        m = tile_of(i)
        gram[2, m, :] = gram[1, :, m].T
        return 0

    lax.fori_loop(0, rows // tile, flip, 0)

    def second(i, _):
        m = tile_of(i)
        total = out[m, :] + matmul(gram[2 * y + 1 - y, m, :], xg[1 - y])
        xp[y, m, :] = total.astype(jnp.bfloat16)
        out[m, :] = (
            quintic_one * xg[y, m, :].astype(jnp.float32) + quintic_three * total
        )
        return 0

    lax.fori_loop(0, rows // tile, second, 0)

    for k in range(nz):
        day[nz + k].wait_recv()
        here = d_slab(1 - y, 1 - xx, lax.rem(z - k + nz, nz))
        dat.append(begin(remote(here, here, dat_s.at[nz + k], dat_r.at[nz + k], to_c)))
    for copy in dat:
        copy.wait_recv()

    def third(i, _):
        m = tile_of(i)
        xp[1 - y, m, :] = (
            matmul(gram[2 * (1 - y) + y, m, :], xg[y])
            + matmul(gram[3 * (1 - y), m, :], xg[1 - y])
        ).astype(jnp.bfloat16)
        return 0

    lax.fori_loop(0, rows // tile, third, 0)

    def back(i):
        m = tile_of(i)
        return pltpu.make_async_copy(out.at[m], o_hbm.at[m], out_sem.at[i])

    def fourth(i, _):
        m = tile_of(i)
        twice = matmul(gram[2 * y, m, :], xp[0]) + matmul(gram[2 * y + 1, m, :], xp[1])
        out[m, :] = (out[m, :] + quintic_five * twice) * scale
        back(i).start()
        return 0

    lax.fori_loop(0, rows // tile, fourth, 0)

    for copy in sends:
        copy.wait_send()

    def finish(i, _):
        back(i).wait()
        return 0

    lax.fori_loop(0, rows // tile, finish, 0)


def fused(mesh, grad_iterate, scale):
    rows, width = grad_iterate.shape
    nz = mesh.shape["fsdp"] // 4
    half, quarter = rows // 2, rows // 4
    dpiece, cpiece = half // nz, quarter // nz
    tile = next(t for t in (256, 128) if rows % t == 0)
    bf16, f32 = jnp.bfloat16, jnp.float32
    dma = pltpu.SemaphoreType.DMA
    scratch = [
        pltpu.VMEM((2, rows, width), bf16),
        pltpu.VMEM((2, rows, width), bf16),
        pltpu.VMEM((4, rows, rows), bf16),
        pltpu.VMEM((rows, width), f32),
        pltpu.VMEM((nz, cpiece, half), f32),
        pltpu.VMEM((nz, dpiece, half), bf16),
        pltpu.VMEM((nz, dpiece, half), bf16),
        pltpu.VMEM((nz - 1, dpiece, half), bf16),
        pltpu.VMEM((nz - 1, dpiece, half), bf16),
        pltpu.VMEM((nz, cpiece, half), bf16),
        pltpu.VMEM((nz, cpiece, half), bf16),
        pltpu.VMEM((nz - 1, cpiece, half), bf16),
        pltpu.VMEM((nz - 1, cpiece, half), bf16),
        dma,
    ]
    pairs = [2, 2, nz, nz - 1, nz, nz - 1, nz - 1, nz, 2 * nz, 2 * nz, 2 * nz,
             None, 2 * (nz - 1), 2 * nz, 4 * nz]
    for count in pairs:
        scratch += [dma if count is None else dma((count,))] * 2
    scratch.append(dma((rows // tile,)))
    flops = 2 * rows * rows * width * 7
    return pl.pallas_call(
        functools.partial(fused_kernel, nz, tile, scale),
        out_shape=jax.ShapeDtypeStruct((rows, width), f32),
        in_specs=[pl.BlockSpec(memory_space=pl.ANY)],
        out_specs=pl.BlockSpec(memory_space=pl.ANY),
        scratch_shapes=scratch,
        compiler_params=pltpu.CompilerParams(
            collective_id=0, has_side_effects=True, vmem_limit_bytes=67043328
        ),
        cost_estimate=pl.CostEstimate(
            flops=flops, bytes_accessed=6 * rows * width, transcendentals=0
        ),
    )(grad_iterate)


def fits(mesh, shape):
    rows, width = shape
    devices = mesh.shape["fsdp"]
    if mesh.shape["tp"] != 2 or devices % 4 or devices < 8:
        return False
    nz = devices // 4
    if rows % 256 or rows // 2 > width or width % 128 or (rows // 4) % (16 * nz):
        return False
    return 12 * rows * width + 8 * rows * rows + 4 * rows * rows < 64 * 2**20


def solution(mesh):
    def local(scale, grad_iterate):
        if fits(mesh, grad_iterate.shape):
            return fused(mesh, grad_iterate, scale)
        return general(grad_iterate, scale)

    def whole(grad_iterate):
        scale = math.sqrt(grad_iterate.shape[1])
        return jax.shard_map(
            functools.partial(local, scale),
            mesh=mesh,
            in_specs=(P("tp", "fsdp"),),
            out_specs=P("tp", "fsdp"),
            check_vma=False,
        )(grad_iterate)

    return whole
```

time: 563 us -> 255 us (0.45)
  waiting for transfers between devices: 358 us -> 0 us
  Pallas kernels: 0 us -> 243 us
  matrix products: 120 us -> 0 us
  local copies, waits for them, and re-layouts: 32.9 us -> 7.22 us
  other arithmetic: 18.5 us -> 0 us
  between operations: 13.9 us -> 0.01 us
  blocking collectives: 7 us -> 0 us
    pallas_call x0 -> x1, Pallas kernels: none -> 243 us  [fused(): pl.pallas_call(functools.partial(fused_kernel, nz, tile, scale), out_shap...]
    dot_general x15 -> x0, matrix products: 120 us -> none  [the longest x12 94.3 us: matmul(): return jnp.dot(a, b, preferred_element_type=jnp.float32)]
    all_gather x3 -> x0, waiting for transfers between devices: 113 us -> none  [the longest x1 46.5 us: paired(): cross = lax.all_gather(cross_share, 'fsdp', axis=0, tiled=True)]
    ppermute x4 -> x0, waiting for transfers between devices: 107 us -> none  [the longest x1 84.3 us: paired(): other = lax.ppermute(own, 'tp', swap)]
    reduce_scatter x2 -> x0, waiting for transfers between devices: 87.2 us -> none  [reduced(): share = lax.psum_scatter(partial, 'fsdp', scatter_dimension=0, tiled=True)]
    unnamed x7 -> x0, waiting for transfers between devices: 51.1 us -> none
    select_n x2 -> x0, other arithmetic: 10.7 us -> none  [the longest x1 8.09 us: paired(): cross = jnp.where(first, cross.T, cross)]
    all_gather x1 -> x0, local copies, waits for them, and re-layouts: 9.98 us -> none  [paired(): cross = lax.all_gather(cross_share, 'fsdp', axis=0, tiled=True)]
  transfers between devices with their start and end apart: 10 -> 0, of which waited for: 7 -> 0; matrix products, arithmetic and copies ran while one was open for 21% -> 0% of each run, Pallas kernels for 0% -> 0%
where the time goes in v1:
time: 255 us; the launch traced here: 250 us
  Pallas kernels  243 us (95%)
  local copies, waits for them, and re-layouts  7.22 us (3%)
    pallas_call x1, Pallas kernels, fused(): pl.pallas_call(functools.partial(fused_kernel, nz, tile, scale), out_shap...  243 us
    unnamed x1, local copies, waits for them, and re-layouts  7.22 us

profile of v1, /device:TPU:28, one launch (start us, length us, event | category | flops | bytes accessed | tf_op | source)
XLA Modules:
  0.0 250.3 jit_solution(11031742992793212808)
XLA Ops:
  0.0 243.0 %shard_map.17 = f32[1792,1152]{1,0:T(8,128)} custom-call(bf16[1792,1152]{1,0:T(8,128)(2,1)} %x_hbm.1), custom_call_target="tpu_custom_call" | custom-call | flops 51791265792 | bytes 12386304 | tf_op jit(solution)/shard_map/pallas_call | solution.py:382
  243.1 7.2 %copy.3 = f32[1792,1152]{1,0:T(8,128)} copy(f32[1792,1152]{1,0:T(8,128)} %shard_map.17) | data formatting | bytes 16515072

commit v2 on v1

v2 whole, which is shorter than its diff:
```python
import functools
import math

import jax
import jax.numpy as jnp
from jax import lax
from jax.experimental import pallas as pl
from jax.experimental.pallas import tpu as pltpu
from jax.sharding import PartitionSpec as P

quintic_one = 3.4445
quintic_three = -4.775
quintic_five = 2.0315

MESH = pl.DeviceIdType.MESH


def rows_by_rows(a, b):
    return lax.dot_general(a, b, (((1,), (1,)), ((), ())), preferred_element_type=jnp.float32)


def columns_by_rows(a, b):
    return lax.dot_general(a, b, (((0,), (0,)), ((), ())), preferred_element_type=jnp.float32)


def matmul(a, b):
    return jnp.dot(a, b, preferred_element_type=jnp.float32)


def general(grad_iterate, scale):
    columns = lax.all_gather(grad_iterate, "tp", axis=0, tiled=True)
    shares = lax.psum_scatter(
        rows_by_rows(columns, grad_iterate), "fsdp", scatter_dimension=0, tiled=True
    )
    gram_cols = lax.all_gather(shares.astype(jnp.bfloat16), "fsdp", axis=0, tiled=True)
    applied = lax.dot_general(
        gram_cols, columns, (((0,), (0,)), ((), ())), preferred_element_type=jnp.float32
    )
    twice_applied = matmul(
        gram_cols.T, lax.all_gather(applied.astype(jnp.bfloat16), "tp", axis=0, tiled=True)
    )
    mixed = (
        quintic_one * grad_iterate.astype(jnp.float32)
        + quintic_three * applied
        + quintic_five * twice_applied
    )
    return mixed * scale


def fused_kernel(
    nz, tile, scale,
    x_hbm, o_hbm,
    xg, xp, gram, acc, dxs, dxr, dzs, dzr, cxs, cxr, czs, czr,
    local_sem, ys, yr, cs, cr, dx_s, dx_r, dz_s, dz_r, cx_s, cx_r, cz_s, cz_r,
    dey_s, dey_r, daz_s, daz_r, dtz_s, dtz_r, dax_s, dax_r, dtx_s, dtx_r,
    dac_s, dac_r, dtc_s, dtc_r, dly_s, dly_r, dlc_s, dlc_r,
    cay_s, cay_r, caz_s, caz_r, cax_s, cax_r, cac_s, cac_r, out_sem,
):
    f = lax.axis_index("fsdp")
    y = lax.axis_index("tp")
    c = lax.rem(f, 2)
    xx = lax.rem(f // 2, 2)
    z = f // 4

    rows = xg.shape[1]
    half = rows // 2
    quarter = half // 2
    dpiece = half // nz
    cpiece = quarter // nz

    def device(z_, x_, c_, y_):
        return (z_ * 4 + x_ * 2 + c_, y_)

    to_y = device(z, xx, c, 1 - y)
    to_x = device(z, 1 - xx, c, y)
    to_c = device(z, xx, 1 - c, y)
    to_z = [device(lax.rem(z + k, nz), xx, c, y) for k in range(1, nz)]

    def remote(src, dst, ssem, rsem, target):
        return pltpu.make_async_remote_copy(
            src_ref=src, dst_ref=dst, send_sem=ssem, recv_sem=rsem,
            device_id=target, device_id_type=MESH,
        )

    load = pltpu.make_async_copy(x_hbm, xg.at[y], local_sem)
    load.start()
    barrier = pltpu.get_barrier_semaphore()
    peers = [to_y, to_x, to_c] + to_z
    for peer in peers:
        pl.semaphore_signal(barrier, inc=1, device_id=peer, device_id_type=MESH)
    pl.semaphore_wait(barrier, len(peers))
    load.wait()

    sends = []

    def begin(copy):
        copy.start()
        sends.append(copy)
        return copy

    def move(block, ssem, rsem, target):
        return begin(remote(block, block, ssem, rsem, target))

    def at(i, n):
        return pl.ds(pl.multiple_of(i, n if n < 128 else 16), n)

    def back_from(k):
        return lax.rem(z - k + nz, nz)

    share = begin(remote(xg.at[y], xp.at[y], cs.at[0], cr.at[0], to_c))

    def x_block(s):
        h = (1 - y) if s < 2 else y
        return xg.at[y, at(h * half + (s % 2) * quarter, quarter)]

    over = [move(x_block(s), ys.at[s], yr.at[s], to_y) for s in range(3)]
    share.wait_recv()

    cols = pl.ds(pl.multiple_of(c * half, 128), half)
    rhs = at(c * half, half)

    def gram_part(left, lrow, n, right):
        l = at(lrow, n)
        return rows_by_rows(xg[left, l, :], xg[right, rhs, :]) + rows_by_rows(
            xp[left, l, :], xp[right, rhs, :]
        )

    def order(p):
        return lax.rem(z + 1 + p, nz)

    def d_copy(p):
        t = order(p)
        return remote(dxs.at[t], dxr.at[t], dx_s.at[p], dx_r.at[p], to_x)

    def d_send(p, _):
        t = order(p)
        dxs[t] = gram_part(y, (1 - xx) * half + t * dpiece, dpiece, y).astype(jnp.bfloat16)
        d_copy(p).start()
        return 0

    lax.fori_loop(0, nz, d_send, 0)

    def d_own(p, _):
        t = order(p)
        acc[y, at(t * dpiece, dpiece), 0:half] = gram_part(
            y, xx * half + t * dpiece, dpiece, y
        )
        return 0

    lax.fori_loop(0, nz, d_own, 0)

    dz = []
    for p in range(nz):
        t = order(p)
        d_copy(p).wait()
        place = at(t * dpiece, dpiece)
        total = acc[y, place, 0:half] + dxr[t].astype(jnp.float32)
        if p < nz - 1:
            dzs[p] = total.astype(jnp.bfloat16)
            dz.append(begin(remote(dzs.at[p], dzr.at[p], dz_s.at[p], dz_r.at[p], to_z[p])))
        else:
            acc[y, place, 0:half] = total

    for s in range(2):
        over[s].wait_recv()
    fwd = (1 - y) * (1 - c) + y
    block = at(fwd * half, half)
    cfwd = remote(xg.at[1 - y, block], xp.at[1 - y, block], cs.at[1], cr.at[1], to_c)
    sends.append(cfwd)
    late_send = jnp.logical_and(y == 0, c == 0)
    late_c = jnp.logical_and(y == 0, c == 1)

    @pl.when(jnp.logical_not(late_send))
    def _():
        cfwd.start()

    def c_copy(t):
        return remote(cxs.at[t], cxr.at[t], cx_s.at[t], cx_r.at[t], to_x)

    def cz_copy(p):
        return remote(czs.at[p], czr.at[p], cz_s.at[p], cz_r.at[p], to_z[p])

    def c_compute():
        cfwd.wait_recv()
        part = gram_part(0, y * half + (1 - xx) * quarter, quarter, 1)
        for t in range(nz):
            cxs[t] = part[t * cpiece:(t + 1) * cpiece].astype(jnp.bfloat16)
        for t in range(nz):
            c_copy(t).start()
        acc[1 - y, 0:quarter, 0:half] = gram_part(0, y * half + xx * quarter, quarter, 1)

    def c_exchange():
        for t in range(nz):
            c_copy(t).wait()
        for p in range(nz - 1):
            t = order(p)
            czs[p] = (
                acc[1 - y, at(t * cpiece, cpiece), 0:half] + cxr[t].astype(jnp.float32)
            ).astype(jnp.bfloat16)
            cz_copy(p).start()

    def c_slab(who, x_, z_):
        return (1, at(who * half + x_ * quarter + z_ * cpiece, cpiece), cols)

    cmine = gram.at[c_slab(y, xx, z)]
    cay = remote(cmine, cmine, cay_s, cay_r, to_y)

    def c_finish():
        total = acc[1 - y, at(z * cpiece, cpiece), 0:half] + cxr[z].astype(jnp.float32)
        for p in range(nz - 1):
            cz_copy(p).wait()
            total = total + czr[p].astype(jnp.float32)
        gram[c_slab(y, xx, z)] = total.astype(jnp.bfloat16)
        cay.start()

    @pl.when(jnp.logical_not(late_c))
    def _():
        c_compute()

    def d_slab(who, x_, z_):
        return (2 * who, at(x_ * half + z_ * dpiece, dpiece), cols)

    def d_part(who, x_, z_, part):
        return (2 * who, at(x_ * half + z_ * dpiece + part * cpiece, cpiece), cols)

    total = acc[y, at(z * dpiece, dpiece), 0:half]
    for p in range(nz - 1):
        dz[p].wait_recv()
        total = total + dzr[p].astype(jnp.float32)
    gram[d_slab(y, xx, z)] = total.astype(jnp.bfloat16)

    dey = move(gram.at[d_part(y, xx, z, 0)], dey_s, dey_r, to_y)
    over.append(move(x_block(3), ys.at[3], yr.at[3], to_y))
    daz, dax, dac, dtz, dtx, dtc, dly, dlc = [], [], [], [], [], [], [], []

    def pass_own(k):
        here = gram.at[d_slab(y, xx, back_from(k))]
        dax.append(move(here, dax_s.at[k], dax_r.at[k], to_x))
        dac.append(move(here, dac_s.at[k], dac_r.at[k], to_c))

    def pass_theirs(k):
        here = gram.at[d_part(1 - y, xx, back_from(k), 0)]
        dtx.append(move(here, dtx_s.at[k], dtx_r.at[k], to_x))
        dtc.append(move(here, dtc_s.at[k], dtc_r.at[k], to_c))

    def pass_late(k, x_):
        here = gram.at[d_part(y, x_, back_from(k % nz), 1)]
        dly.append(move(here, dly_s.at[k], dly_r.at[k], to_y))

    dmine = gram.at[d_slab(y, xx, z)]

    def spread_own(k):
        daz.append(move(dmine, daz_s.at[k], daz_r.at[k], to_z[k]))

    pass_own(0)
    spread_own(0)

    @pl.when(jnp.logical_not(late_c))
    def _():
        c_exchange()

    for k in range(1, nz - 1):
        spread_own(k)
    dey.wait_recv()
    dtheirs = gram.at[d_part(1 - y, xx, z, 0)]
    for k in range(nz - 1):
        dtz.append(move(dtheirs, dtz_s.at[k], dtz_r.at[k], to_z[k]))
    daz[0].wait_recv()
    pass_own(1)
    pass_theirs(0)

    @pl.when(jnp.logical_not(late_c))
    def _():
        c_finish()

    pass_late(0, xx)
    pass_late(1, xx)
    def c_move(who, k, target, ssem, rsem):
        here = gram.at[c_slab(who, xx, back_from(k))]
        return remote(here, here, ssem, rsem, target)

    def c_over_z(who, k):
        j = who * (nz - 1) + k
        return c_move(who, 0, to_z[k], caz_s.at[j], caz_r.at[j])

    def c_over_x(who, k):
        j = who * nz + k
        return c_move(who, k, to_x, cax_s.at[j], cax_r.at[j])

    def c_over_c(who, k):
        j = who * nz + k
        return c_move(who, k, to_c, cac_s.at[j], cac_r.at[j])

    def c_spread(who):
        @pl.when(y == 1 - who)
        def _():
            cay.wait_recv()

        for k in range(nz - 1):
            c_over_z(who, k).start()
        c_over_x(who, 0).start()
        c_over_c(who, 0).start()

    for s in range(2, 4):
        over[s].wait_recv()

    @pl.when(late_send)
    def _():
        cfwd.start()

    @pl.when(late_c)
    def _():
        c_compute()

    c_spread(1)

    @pl.when(c == 0)
    def _():
        c_spread(0)

    for k in range(2, nz):
        daz[k - 1].wait_recv()
        pass_own(k)
        pass_late(k, xx)

    @pl.when(late_c)
    def _():
        c_exchange()

    dtz[0].wait_recv()
    pass_theirs(1)

    def d_from_x(k):
        dax[k].wait_recv()
        here = gram.at[d_slab(y, 1 - xx, back_from(k))]
        dac.append(move(here, dac_s.at[nz + k], dac_r.at[nz + k], to_c))
        pass_late(nz + k, 1 - xx)

    d_from_x(0)
    for k in range(2, nz):
        dtz[k - 1].wait_recv()
        pass_theirs(k)
        d_from_x(k - 1)

    @pl.when(late_c)
    def _():
        c_finish()

    d_from_x(nz - 1)

    @pl.when(c == 1)
    def _():
        c_spread(0)

    for k in range(nz):
        dtx[k].wait_recv()
        here = gram.at[d_part(1 - y, 1 - xx, back_from(k), 0)]
        dtc.append(move(here, dtc_s.at[nz + k], dtc_r.at[nz + k], to_c))
    for copy in dac:
        copy.wait_recv()

    def tile_of(i):
        return at(i * tile, tile)

    tiles = rows // tile

    def diagonal(side, first, count):
        def body(i, _):
            m = tile_of(i)
            acc[side, m, :] = matmul(gram[2 * side, m, :], xg[side])
            return 0

        lax.fori_loop(first, first + count, body, 0)

    def share_out(side, events):
        done = 0
        for n, event in enumerate(events):
            upto = tiles * (n + 1) // len(events)
            if upto > done:
                diagonal(side, done, upto - done)
            done = upto
            event()

    def c_pass(who, k):
        def event():
            c_over_z(who, k - 1).wait_recv()
            c_over_x(who, k).start()
            c_over_c(who, k).start()

        return event

    def d_late(k):
        def event():
            dly[k].wait_recv()
            here = gram.at[d_part(1 - y, xx if k < nz else 1 - xx, back_from(k % nz), 1)]
            dlc.append(move(here, dlc_s.at[k], dlc_r.at[k], to_c))

        return event

    def c_from_x(who, k):
        def event():
            c_over_x(who, k).wait_recv()
            j = (2 + who) * nz + k
            here = gram.at[c_slab(who, 1 - xx, back_from(k))]
            far[who].append(move(here, cac_s.at[j], cac_r.at[j], to_c))

        return event

    def cross(x_, who, last):
        m = at(who * half + x_ * quarter, quarter)
        total = acc[0, m, :] + matmul(gram[1, m, :], xg[1])
        acc[0, m, :] = total
        xp[0, m, :] = total.astype(jnp.bfloat16)

        def body(i, _):
            n = tile_of(i)
            ncol = pl.ds(pl.multiple_of(i * tile, 128), tile)
            total = acc[1, n, :] + columns_by_rows(gram[1, m, ncol], xg[0, m, :])
            acc[1, n, :] = total
            if last:
                xp[1, n, :] = total.astype(jnp.bfloat16)
            return 0

        lax.fori_loop(0, tiles, body, 0)

    def cross_own(who):
        for k in range(nz):
            c_over_c(who, k).wait_recv()
        cross(xx, who, False)

    def cross_far(who, last):
        for copy in far[who]:
            copy.wait_recv()
        cross(1 - xx, who, last)

    far = [[], []]
    share_out(y, [c_pass(1, k) for k in range(1, nz)])
    for k in range(2 * nz):
        d_late(k)()
    for copy in dtc + dlc:
        copy.wait_recv()
    share_out(
        1 - y,
        [c_from_x(1, k) for k in range(nz)] + [c_pass(0, k) for k in range(1, nz)],
    )
    cross_own(1)
    cross_far(1, False)
    for k in range(nz):
        c_from_x(0, k)()
    cross_own(0)
    cross_far(0, True)

    def back(i):
        m = tile_of(i)
        return pltpu.make_async_copy(acc.at[y, m], o_hbm.at[m], out_sem.at[i])

    def finish(m, twice):
        acc[y, m, :] = (
            quintic_one * xg[y, m, :].astype(jnp.float32)
            + quintic_three * acc[y, m, :]
            + quintic_five * twice
        ) * scale

    @pl.when(y == 0)
    def _():
        def body(i, _):
            m = tile_of(i)
            finish(m, matmul(gram[0, m, :], xp[0]) + matmul(gram[1, m, :], xp[1]))
            back(i).start()
            return 0

        lax.fori_loop(0, rows // tile, body, 0)

    @pl.when(y == 1)
    def _():
        def body(i, _):
            m = tile_of(i)
            ncol = pl.ds(pl.multiple_of(i * tile, 128), tile)
            finish(m, columns_by_rows(gram[1, :, ncol], xp[0]) + matmul(gram[2, m, :], xp[1]))
            back(i).start()
            return 0

        lax.fori_loop(0, rows // tile, body, 0)

    for who in range(2):
        for k in range(nz - 1):
            sends.append(c_over_z(who, k))
        for k in range(nz):
            sends += [c_over_x(who, k), c_over_c(who, k)]
    for copy in sends + [cay]:
        copy.wait_send()

    def drain(i, _):
        back(i).wait()
        return 0

    lax.fori_loop(0, rows // tile, drain, 0)


def fused(mesh, grad_iterate, scale):
    rows, width = grad_iterate.shape
    nz = mesh.shape["fsdp"] // 4
    half, quarter = rows // 2, rows // 4
    dpiece, cpiece = half // nz, quarter // nz
    tile = next(t for t in (256, 128) if rows % t == 0)
    bf16, f32 = jnp.bfloat16, jnp.float32
    dma = pltpu.SemaphoreType.DMA
    scratch = [
        pltpu.VMEM((2, rows, width), bf16),
        pltpu.VMEM((2, rows, width), bf16),
        pltpu.VMEM((3, rows, rows), bf16),
        pltpu.VMEM((2, rows, width), f32),
        pltpu.VMEM((nz, dpiece, half), bf16),
        pltpu.VMEM((nz, dpiece, half), bf16),
        pltpu.VMEM((nz - 1, dpiece, half), bf16),
        pltpu.VMEM((nz - 1, dpiece, half), bf16),
        pltpu.VMEM((nz, cpiece, half), bf16),
        pltpu.VMEM((nz, cpiece, half), bf16),
        pltpu.VMEM((nz - 1, cpiece, half), bf16),
        pltpu.VMEM((nz - 1, cpiece, half), bf16),
        dma,
    ]
    counts = dict(
        y=4, c=2, dx=nz, dz=nz - 1, cx=nz, cz=nz - 1, dey=None, daz=nz - 1, dtz=nz - 1,
        dax=nz, dtx=nz, dac=2 * nz, dtc=2 * nz, dly=2 * nz, dlc=2 * nz,
        cay=None, caz=2 * (nz - 1), cax=2 * nz, cac=4 * nz,
    )
    for count in counts.values():
        scratch += [dma if count is None else dma((count,))] * 2
    scratch.append(dma((rows // tile,)))
    flops = 2 * rows * rows * width * 7
    return pl.pallas_call(
        functools.partial(fused_kernel, nz, tile, scale),
        out_shape=jax.ShapeDtypeStruct((rows, width), f32),
        in_specs=[pl.BlockSpec(memory_space=pl.ANY)],
        out_specs=pl.BlockSpec(memory_space=pl.ANY),
        scratch_shapes=scratch,
        compiler_params=pltpu.CompilerParams(
            collective_id=0, has_side_effects=True, vmem_limit_bytes=67043328
        ),
        cost_estimate=pl.CostEstimate(
            flops=flops, bytes_accessed=6 * rows * width, transcendentals=0
        ),
    )(grad_iterate)


def fits(mesh, shape):
    rows, width = shape
    devices = mesh.shape["fsdp"]
    if mesh.shape["tp"] != 2 or devices % 4 or devices < 8:
        return False
    nz = devices // 4
    if rows % 256 or rows // 2 > width or width % 128 or (rows // 4) % (16 * nz):
        return False
    return 16 * rows * width + 8 * rows * rows < 60 * 2**20


def solution(mesh):
    def local(scale, grad_iterate):
        if fits(mesh, grad_iterate.shape):
            return fused(mesh, grad_iterate, scale)
        return general(grad_iterate, scale)

    def whole(grad_iterate):
        scale = math.sqrt(grad_iterate.shape[1])
        return jax.shard_map(
            functools.partial(local, scale),
            mesh=mesh,
            in_specs=(P("tp", "fsdp"),),
            out_specs=P("tp", "fsdp"),
            check_vma=False,
        )(grad_iterate)

    return whole
```

time: 255 us -> 246 us (0.965); the launches traced: 250 us -> 246 us
  Pallas kernels: 243 us -> 239 us
    pallas_call x1, Pallas kernels: 243 us -> 239 us  [fused(): pl.pallas_call(functools.partial(fused_kernel, nz, tile, scale), out_shap...]
where the time goes in v2:
time: 246 us
  Pallas kernels  239 us (97%)
  local copies, waits for them, and re-layouts  7.22 us (3%)
    pallas_call x1, Pallas kernels, fused(): pl.pallas_call(functools.partial(fused_kernel, nz, tile, scale), out_shap...  239 us
    unnamed x1, local copies, waits for them, and re-layouts  7.22 us

profile of v2, /device:TPU:28, one launch (start us, length us, event | category | flops | bytes accessed | tf_op | source)
XLA Modules:
  0.0 246.1 jit_solution(9972224688152992254)
XLA Ops:
  0.0 238.9 %shard_map.17 = f32[1792,1152]{1,0:T(8,128)} custom-call(bf16[1792,1152]{1,0:T(8,128)(2,1)} %x_hbm.1), custom_call_target="tpu_custom_call" | custom-call | flops 51791265792 | bytes 12386304 | tf_op jit(solution)/shard_map/pallas_call | solution.py:532
  238.9 7.2 %copy.3 = f32[1792,1152]{1,0:T(8,128)} copy(f32[1792,1152]{1,0:T(8,128)} %shard_map.17) | data formatting | bytes 16515072

commit v3 on v2

--- a/solution.py
+++ b/solution.py
@@ -52,8 +52,7 @@
     x_hbm, o_hbm,
     xg, xp, gram, acc, dxs, dxr, dzs, dzr, cxs, cxr, czs, czr,
     local_sem, ys, yr, cs, cr, dx_s, dx_r, dz_s, dz_r, cx_s, cx_r, cz_s, cz_r,
-    dey_s, dey_r, daz_s, daz_r, dtz_s, dtz_r, dax_s, dax_r, dtx_s, dtx_r,
-    dac_s, dac_r, dtc_s, dtc_r, dly_s, dly_r, dlc_s, dlc_r,
+    daz_s, daz_r, dax_s, dax_r, dac_s, dac_r, dly_s, dly_r, dlc_s, dlc_r,
     cay_s, cay_r, caz_s, caz_r, cax_s, cax_r, cac_s, cac_r, out_sem,
 ):
     f = lax.axis_index("fsdp")
@@ -113,7 +112,7 @@
         h = (1 - y) if s < 2 else y
         return xg.at[y, at(h * half + (s % 2) * quarter, quarter)]
 
-    over = [move(x_block(s), ys.at[s], yr.at[s], to_y) for s in range(3)]
+    over = [move(x_block(s), ys.at[s], yr.at[s], to_y) for s in range(4)]
     share.wait_recv()
 
     cols = pl.ds(pl.multiple_of(c * half, 128), half)
@@ -220,31 +219,21 @@
     def d_slab(who, x_, z_):
         return (2 * who, at(x_ * half + z_ * dpiece, dpiece), cols)
 
-    def d_part(who, x_, z_, part):
-        return (2 * who, at(x_ * half + z_ * dpiece + part * cpiece, cpiece), cols)
-
     total = acc[y, at(z * dpiece, dpiece), 0:half]
     for p in range(nz - 1):
         dz[p].wait_recv()
         total = total + dzr[p].astype(jnp.float32)
     gram[d_slab(y, xx, z)] = total.astype(jnp.bfloat16)
 
-    dey = move(gram.at[d_part(y, xx, z, 0)], dey_s, dey_r, to_y)
-    over.append(move(x_block(3), ys.at[3], yr.at[3], to_y))
-    daz, dax, dac, dtz, dtx, dtc, dly, dlc = [], [], [], [], [], [], [], []
+    daz, dax, dac, dly, dlc = [], [], [], [], []
 
     def pass_own(k):
         here = gram.at[d_slab(y, xx, back_from(k))]
         dax.append(move(here, dax_s.at[k], dax_r.at[k], to_x))
         dac.append(move(here, dac_s.at[k], dac_r.at[k], to_c))
 
-    def pass_theirs(k):
-        here = gram.at[d_part(1 - y, xx, back_from(k), 0)]
-        dtx.append(move(here, dtx_s.at[k], dtx_r.at[k], to_x))
-        dtc.append(move(here, dtc_s.at[k], dtc_r.at[k], to_c))
-
-    def pass_late(k, x_):
-        here = gram.at[d_part(y, x_, back_from(k % nz), 1)]
+    def pass_late(k):
+        here = gram.at[d_slab(y, xx if k < nz else 1 - xx, back_from(k % nz))]
         dly.append(move(here, dly_s.at[k], dly_r.at[k], to_y))
 
     dmine = gram.at[d_slab(y, xx, z)]
@@ -261,20 +250,16 @@
 
     for k in range(1, nz - 1):
         spread_own(k)
-    dey.wait_recv()
-    dtheirs = gram.at[d_part(1 - y, xx, z, 0)]
-    for k in range(nz - 1):
-        dtz.append(move(dtheirs, dtz_s.at[k], dtz_r.at[k], to_z[k]))
     daz[0].wait_recv()
     pass_own(1)
-    pass_theirs(0)
 
     @pl.when(jnp.logical_not(late_c))
     def _():
         c_finish()
 
-    pass_late(0, xx)
-    pass_late(1, xx)
+    pass_late(0)
+    pass_late(1)
+
     def c_move(who, k, target, ssem, rsem):
         here = gram.at[c_slab(who, xx, back_from(k))]
         return remote(here, here, ssem, rsem, target)
@@ -321,41 +306,34 @@
     for k in range(2, nz):
         daz[k - 1].wait_recv()
         pass_own(k)
-        pass_late(k, xx)
+        pass_late(k)
 
     @pl.when(late_c)
     def _():
         c_exchange()
-
-    dtz[0].wait_recv()
-    pass_theirs(1)
 
     def d_from_x(k):
         dax[k].wait_recv()
         here = gram.at[d_slab(y, 1 - xx, back_from(k))]
         dac.append(move(here, dac_s.at[nz + k], dac_r.at[nz + k], to_c))
-        pass_late(nz + k, 1 - xx)
-
-    d_from_x(0)
-    for k in range(2, nz):
-        dtz[k - 1].wait_recv()
-        pass_theirs(k)
-        d_from_x(k - 1)
+
+    for k in range(nz - 1):
+        d_from_x(k)
+    pass_late(nz)
 
     @pl.when(late_c)
     def _():
         c_finish()
 
+    for k in range(1, nz - 1):
+        pass_late(nz + k)
+
+    @pl.when(c == 1)
+    def _():
+        c_spread(0)
+
     d_from_x(nz - 1)
-
-    @pl.when(c == 1)
-    def _():
-        c_spread(0)
-
-    for k in range(nz):
-        dtx[k].wait_recv()
-        here = gram.at[d_part(1 - y, 1 - xx, back_from(k), 0)]
-        dtc.append(move(here, dtc_s.at[nz + k], dtc_r.at[nz + k], to_c))
+    pass_late(2 * nz - 1)
     for copy in dac:
         copy.wait_recv()
 
@@ -364,20 +342,26 @@
 
     tiles = rows // tile
 
-    def diagonal(side, first, count):
+    def clear(i, _):
+        acc[1 - y, tile_of(i), :] = jnp.zeros((tile, acc.shape[2]), jnp.float32)
+        return 0
+
+    lax.fori_loop(0, tiles, clear, 0)
+
+    def diagonal(first, count):
         def body(i, _):
             m = tile_of(i)
-            acc[side, m, :] = matmul(gram[2 * side, m, :], xg[side])
+            acc[y, m, :] = matmul(gram[2 * y, m, :], xg[y])
             return 0
 
         lax.fori_loop(first, first + count, body, 0)
 
-    def share_out(side, events):
+    def share_out(events):
         done = 0
         for n, event in enumerate(events):
             upto = tiles * (n + 1) // len(events)
             if upto > done:
-                diagonal(side, done, upto - done)
+                diagonal(done, upto - done)
             done = upto
             event()
 
@@ -390,12 +374,16 @@
         return event
 
     def d_late(k):
-        def event():
-            dly[k].wait_recv()
-            here = gram.at[d_part(1 - y, xx if k < nz else 1 - xx, back_from(k % nz), 1)]
-            dlc.append(move(here, dlc_s.at[k], dlc_r.at[k], to_c))
-
-        return event
+        dly[k].wait_recv()
+        here = gram.at[d_slab(1 - y, xx if k < nz else 1 - xx, back_from(k % nz))]
+        dlc.append(move(here, dlc_s.at[k], dlc_r.at[k], to_c))
+
+    def d_other(k):
+        dlc[k].wait_recv()
+        r = at((xx if k < nz else 1 - xx) * half + back_from(k % nz) * dpiece, dpiece)
+        total = acc[1 - y, r, :] + matmul(gram[2 * (1 - y), r, :], xg[1 - y])
+        acc[1 - y, r, :] = total
+        xp[1 - y, r, :] = total.astype(jnp.bfloat16)
 
     def c_from_x(who, k):
         def event():
@@ -434,53 +422,65 @@
         cross(1 - xx, who, last)
 
     far = [[], []]
-    share_out(y, [c_pass(1, k) for k in range(1, nz)])
-    for k in range(2 * nz):
-        d_late(k)()
-    for copy in dtc + dlc:
-        copy.wait_recv()
-    share_out(
-        1 - y,
-        [c_from_x(1, k) for k in range(nz)] + [c_pass(0, k) for k in range(1, nz)],
-    )
+    share_out([c_pass(1, k) for k in range(1, nz)])
+    for k in range(1, nz):
+        c_pass(0, k)()
+    for k in range(nz):
+        c_from_x(1, k)()
+    for k in range(nz):
+        d_late(k)
     cross_own(1)
     cross_far(1, False)
     for k in range(nz):
         c_from_x(0, k)()
+    for k in range(nz):
+        d_other(k)
+    for k in range(nz, 2 * nz - 2):
+        d_late(k)
     cross_own(0)
     cross_far(0, True)
+    for k in range(nz, 2 * nz - 2):
+        d_other(k)
+    def near(i, _):
+        m = tile_of(i)
+        acc[y, m, :] = (
+            quintic_one * xg[y, m, :].astype(jnp.float32)
+            + quintic_three * acc[y, m, :]
+            + quintic_five * matmul(gram[2 * y, m, :], xp[y])
+        )
+        return 0
+
+    lax.fori_loop(0, tiles, near, 0)
+    for k in range(2 * nz - 2, 2 * nz):
+        d_late(k)
+        d_other(k)
 
     def back(i):
         m = tile_of(i)
         return pltpu.make_async_copy(acc.at[y, m], o_hbm.at[m], out_sem.at[i])
 
-    def finish(m, twice):
-        acc[y, m, :] = (
-            quintic_one * xg[y, m, :].astype(jnp.float32)
-            + quintic_three * acc[y, m, :]
-            + quintic_five * twice
-        ) * scale
-
     @pl.when(y == 0)
     def _():
         def body(i, _):
             m = tile_of(i)
-            finish(m, matmul(gram[0, m, :], xp[0]) + matmul(gram[1, m, :], xp[1]))
+            acc[0, m, :] = (acc[0, m, :] + quintic_five * matmul(gram[1, m, :], xp[1])) * scale
             back(i).start()
             return 0
 
-        lax.fori_loop(0, rows // tile, body, 0)
+        lax.fori_loop(0, tiles, body, 0)
 
     @pl.when(y == 1)
     def _():
         def body(i, _):
             m = tile_of(i)
             ncol = pl.ds(pl.multiple_of(i * tile, 128), tile)
-            finish(m, columns_by_rows(gram[1, :, ncol], xp[0]) + matmul(gram[2, m, :], xp[1]))
+            acc[1, m, :] = (
+                acc[1, m, :] + quintic_five * columns_by_rows(gram[1, :, ncol], xp[0])
+            ) * scale
             back(i).start()
             return 0
 
-        lax.fori_loop(0, rows // tile, body, 0)
+        lax.fori_loop(0, tiles, body, 0)
 
     for who in range(2):
         for k in range(nz - 1):
@@ -521,8 +521,8 @@
         dma,
     ]
     counts = dict(
-        y=4, c=2, dx=nz, dz=nz - 1, cx=nz, cz=nz - 1, dey=None, daz=nz - 1, dtz=nz - 1,
-        dax=nz, dtx=nz, dac=2 * nz, dtc=2 * nz, dly=2 * nz, dlc=2 * nz,
+        y=4, c=2, dx=nz, dz=nz - 1, cx=nz, cz=nz - 1, daz=nz - 1,
+        dax=nz, dac=2 * nz, dly=2 * nz, dlc=2 * nz,
         cay=None, caz=2 * (nz - 1), cax=2 * nz, cac=4 * nz,
     )
     for count in counts.values():

time: 246 us -> 246 us (level)
  the two profiles are of different devices: /device:TPU:28 before, /device:TPU:30 now
where the time goes in v3:
time: 246 us
  Pallas kernels  238 us (97%)
  local copies, waits for them, and re-layouts  7.22 us (3%)
    pallas_call x1, Pallas kernels, fused(): pl.pallas_call(functools.partial(fused_kernel, nz, tile, scale), out_shap...  238 us
    unnamed x1, local copies, waits for them, and re-layouts  7.22 us

profile of v3, /device:TPU:30, one launch (start us, length us, event | category | flops | bytes accessed | tf_op | source)
XLA Modules:
  0.0 245.6 jit_solution(1620699521020849218)
XLA Ops:
  0.0 238.4 %shard_map.17 = f32[1792,1152]{1,0:T(8,128)} custom-call(bf16[1792,1152]{1,0:T(8,128)(2,1)} %x_hbm.1), custom_call_target="tpu_custom_call" | custom-call | flops 51791265792 | bytes 12386304 | tf_op jit(solution)/shard_map/pallas_call | solution.py:532
  238.4 7.2 %copy.3 = f32[1792,1152]{1,0:T(8,128)} copy(f32[1792,1152]{1,0:T(8,128)} %shard_map.17) | data formatting | bytes 16515072
